TPU v7x, 32 devices: a whole 2x2x4 slice. The times are simulated.
32 devices in a mesh: ent: 2 (over x), blk: 4 (over y, core), rel: 4 (over z).
Axes of the slice: x: 2, y: 2, z: 4, core: 2. Of those that a mesh axis runs over, the one named last changes fastest.
Arguments:
- factors: bfloat16 [8192, 256], P(('ent', 'blk')), may hold values from -12 to 12
- heads: int32 [8, 4, 1, 8192], P(None, 'rel', None, ('ent', 'blk')), may hold values from 0 to 1023, as said below
- tails: int32 [8, 4, 1, 8192], P(None, 'rel', None, ('ent', 'blk')), may hold values from 0 to 1023, as said below
- values: float32 [8, 4, 1, 8192], P(None, 'rel', None, ('ent', 'blk')), may hold values from 0.3 to 9
Outputs:
- relation_fit: float32 [32, 256, 256], P(('ent', 'blk', 'rel'))
- residual: float32 [32, 256, 256], P(('ent', 'blk', 'rel'))
Inputs may be any that keep to these rules, and one draw needn't show every extreme that they name: In every aligned tile of 128 triple columns (columns 128 t to 128 t + 127 of one relation) all heads lie in one aligned block of 128 positions (128 b to 128 b + 127). In every aligned tile of 128 triple columns all tails lie in one aligned block of 128 positions.
All inputs are finite; a program needn't handle non-finite values.
Results may differ from a plain program's by a relative error of at most 0.0029.
Values sent between devices are 32-bit elements; how exact they have to be, the bound alone decides.
A program may use at most 128 MiB of HBM per device.

v0:
```python
import math
import jax
import jax.numpy as jnp
from jax import lax
from jax.sharding import PartitionSpec as P

ITERS = 8
ridge_weight = 0.01
tile_width = 128


def apply_normal(gram_matrix, stacked):
    left_side = jnp.einsum("ab,kbc->kac", gram_matrix, stacked, precision=lax.Precision.HIGHEST)
    return (
        jnp.einsum("kac,cd->kad", left_side, gram_matrix, precision=lax.Precision.HIGHEST)
        + ridge_weight * stacked
    )


def two_products(residual, image_map):
    return lax.psum(
        (jnp.sum(residual * residual), jnp.sum(residual * image_map)), ("ent", "blk", "rel")
    )


def select_rows(entity_ids, block_table):
    group_size, width = entity_ids.shape
    tile_count = width // tile_width
    block_count = block_table.shape[0]
    tiled_ids = entity_ids.reshape(group_size, tile_count, tile_width)
    block_of = tiled_ids[:, :, 0] // tile_width
    block_pick = (
        block_of[:, :, None] == jnp.arange(block_count, dtype=jnp.int32)[None, None, :]
    ).astype(jnp.bfloat16)
    chosen = jnp.einsum(
        "gtb,bcr->gtcr", block_pick, block_table, preferred_element_type=jnp.float32
    ).astype(jnp.bfloat16)
    inside = tiled_ids % tile_width
    slot_pick = (
        inside[:, :, :, None] == jnp.arange(tile_width, dtype=jnp.int32)[None, None, None, :]
    ).astype(jnp.bfloat16)
    return jnp.einsum("gtoc,gtcr->gtor", slot_pick, chosen, preferred_element_type=jnp.float32)


def body(factors, heads, tails, values):
    shards = lax.axis_size(("ent", "blk"))
    ent_dev = factors.shape[0]
    rank_width = factors.shape[1]
    triple_count = heads.shape[3]
    relation_rows = heads.shape[0] * heads.shape[2]
    norm_scale = 1.0 / math.sqrt(shards * triple_count)
    gram_total = lax.psum(
        jnp.dot(factors.T, factors, preferred_element_type=jnp.float32), ("ent", "blk")
    )
    gram_matrix = gram_total / (ent_dev * shards)
    block_table = factors.reshape(ent_dev // tile_width, tile_width, rank_width)
    head_ids = heads.reshape(relation_rows, triple_count)
    tail_ids = tails.reshape(relation_rows, triple_count)
    weights = values.reshape(relation_rows, triple_count)

    def grouped(operands):
        head_group, tail_group, weight_group = operands
        group_size = head_group.shape[0]
        tile_count = triple_count // tile_width
        head_rows = select_rows(head_group, block_table)
        weighted = (
            weight_group.reshape(group_size, tile_count, tile_width)[:, :, :, None] * head_rows
        ).astype(jnp.bfloat16)
        tail_rows = select_rows(tail_group, block_table).astype(jnp.bfloat16)
        product = jnp.einsum(
            "gtci,gtcj->gij", weighted, tail_rows, preferred_element_type=jnp.float32
        )
        return product * norm_scale

    own_rows = relation_rows // shards
    group_size = math.gcd(own_rows * lax.axis_size(("ent", "blk")), 4)
    group_total = own_rows * lax.axis_size(("ent", "blk")) // group_size
    shaped = (
        head_ids.reshape(group_total, group_size, triple_count),
        tail_ids.reshape(group_total, group_size, triple_count),
        weights.reshape(group_total, group_size, triple_count),
    )
    results = lax.map(grouped, shaped)
    target = lax.psum_scatter(
        results.reshape(own_rows * lax.axis_size(("ent", "blk")), rank_width, rank_width),
        ("ent", "blk"),
        scatter_dimension=0,
        tiled=True,
    )
    fitted = jnp.zeros_like(target)
    residual = target
    image_map = apply_normal(gram_matrix, residual)
    norm_now, product = two_products(residual, image_map)
    step_size = norm_now / product
    direction = residual
    along = image_map
    for step_index in range(ITERS):
        fitted = fitted + step_size * direction
        residual = residual - step_size * along
        if step_index + 1 < ITERS:
            image_map = apply_normal(gram_matrix, residual)
            norm_next, product = two_products(residual, image_map)
            ratio_next = norm_next / norm_now
            step_size = norm_next / (product - ratio_next * norm_next / step_size)
            direction = residual + ratio_next * direction
            along = image_map + ratio_next * along
            norm_now = norm_next
    return (fitted, residual)


def solution(mesh):
    placed = (
        P(("ent", "blk"), None),
        P(None, "rel", None, ("ent", "blk")),
        P(None, "rel", None, ("ent", "blk")),
        P(None, "rel", None, ("ent", "blk")),
    )
    return jax.shard_map(
        body,
        mesh=mesh,
        in_specs=placed,
        out_specs=(P(("ent", "blk", "rel"), None, None), P(("ent", "blk", "rel"), None, None)),
        check_vma=False,
    )
```

profile of v0, /device:TPU:0, one launch (start us, length us, event | category | flops | bytes accessed | tf_op | source)
XLA Modules:
  0.0 491.8 jit_solution(14854573454437355438)
XLA Ops:
  7.2 0.0 copy-start.1
  7.2 0.0 copy-start.3
  7.2 0.0 all-reduce.10.cloned.1.call-start
  7.2 2.3 fusion.80
  9.5 0.0 all-reduce.10.cloned.1.call-update
  9.5 0.0 reduce-scatter.2.cloned.1.call-start
  9.6 0.8 reduce.2
  10.5 0.8 reduce.3
  11.3 0.0 copy-done.1
  11.3 0.3 copy.14
  11.6 0.0 copy-done.3
  11.6 0.1 reduce.4
  11.7 17.5 %while.13 = (s32[]{:T(128)}, f32[2,4,256,256]{3,2,1,0:T(8,128)}, f32[2,4,1024]{2,1,0:T(4,128)S(1)}, s32[2,4,1024]{2,1,0:T(4,128)S(1)}, bf16[8,128,256]{2,0,1:T(8...) while((s32[]{:T(128)}, f32[2,4,256,256]{3,2,1,0:T(8,128)}, f32[2,4,1024]{2,1,0:T(4,128)S(1)}, ...), condition=%wide.region_1.2_spmd, body=%wide.region_0.0_spmd.sunk | while | flops 1113941504 | bytes 14992225 | solution.py:83
  11.8 0.2 fusion.111
  11.9 0.7 convolution_convert_fusion.4
  12.7 2.7 multiply_convert_fusion.2
  15.5 0.2 fusion.112
  15.6 0.7 convolution_convert_fusion.5
  16.4 4.1 fusion.113
  20.5 0.2 fusion.111
  20.7 0.7 convolution_convert_fusion.4
  21.5 2.7 multiply_convert_fusion.2
  24.2 0.2 fusion.112
  24.4 0.7 convolution_convert_fusion.5
  25.1 4.1 fusion.113
  29.3 0.0 reduce-scatter.2.cloned.1.call-update
  29.3 39.0 %all-reduce.10.cloned.1.call-done = f32[256,256]{1,0:T(8,128)} async-done(((f32[256,256]{1,0:T(8,128)}), f32[256,256]{1,0:T(8,128)}) %all-reduce.10.cloned.1.call-update) | async-done | bytes 262160 | tf_op jit(solution)/shard_map/psum | solution.py:52
  68.3 43.8 %reduce-scatter.2.cloned.1.call-done = f32[1,256,256]{2,1,0:T(8,128)} async-done(((f32[8,256,256]{2,1,0:T(8,128)}), f32[1,256,256]{2,1,0:T(8,128)}) %reduce-scatter.2.cloned.1.call-update) | async-done | bytes 262160 | tf_op jit(solution)/shard_map/reduce_scatter | solution.py:84
  112.1 1.6 convolution_bitcast_fusion.15
  113.7 2.2 multiply_reduce_fusion.14
  116.0 39.5 %all-reduce.7 = (f32[]{:T(128)}, f32[]{:T(128)}) all-reduce(f32[]{:T(128)} %get-tuple-element.128, f32[]{:T(128)} %get-tuple-element.127), channel_id=1, replica_groups=mesh['ent'=2,'blk'=4,'rel'=4] {'ent','blk','rel'}, use_global_device_ids=true, to_apply=%region_4.5 | all-reduce | flops 2 | bytes 16 | tf_op jit(solution)/shard_map/psum | solution.py:21
  156.8 1.0 multiply_subtract_fusion.7
  157.8 0.0 copy-done
  157.8 0.6 convolution_bitcast_fusion.13
  158.4 1.3 multiply_reduce_fusion.12
  159.7 41.4 %all-reduce.6 = (f32[]{:T(128)}, f32[]{:T(128)}) all-reduce(f32[]{:T(128)} %get-tuple-element.126, f32[]{:T(128)} %get-tuple-element.125), channel_id=1, replica_groups=mesh['ent'=2,'blk'=4,'rel'=4] {'ent','blk','rel'}, use_global_device_ids=true, to_apply=%region_9.10 | all-reduce | flops 2 | bytes 16 | tf_op jit(solution)/shard_map/psum | solution.py:21
  205.5 0.1 multiply_subtract_fusion.6
  205.5 0.6 convolution_bitcast_fusion.11
  206.1 1.2 multiply_reduce_fusion.10
  207.3 39.6 %all-reduce.5 = (f32[]{:T(128)}, f32[]{:T(128)}) all-reduce(f32[]{:T(128)} %get-tuple-element.124, f32[]{:T(128)} %get-tuple-element.123), channel_id=1, replica_groups=mesh['ent'=2,'blk'=4,'rel'=4] {'ent','blk','rel'}, use_global_device_ids=true, to_apply=%region_13.14 | all-reduce | flops 2 | bytes 16 | tf_op jit(solution)/shard_map/psum | solution.py:21
  250.7 0.1 multiply_subtract_fusion.5
  250.7 0.6 convolution_bitcast_fusion.9
  251.3 1.3 multiply_reduce_fusion.8
  252.6 41.5 %all-reduce.4 = (f32[]{:T(128)}, f32[]{:T(128)}) all-reduce(f32[]{:T(128)} %get-tuple-element.122, f32[]{:T(128)} %get-tuple-element.121), channel_id=1, replica_groups=mesh['ent'=2,'blk'=4,'rel'=4] {'ent','blk','rel'}, use_global_device_ids=true, to_apply=%region_17.18 | all-reduce | flops 2 | bytes 16 | tf_op jit(solution)/shard_map/psum | solution.py:21
  298.1 0.1 multiply_subtract_fusion.4
  298.1 0.6 convolution_bitcast_fusion.7
  298.7 1.2 multiply_reduce_fusion.6
  299.9 39.6 %all-reduce.3 = (f32[]{:T(128)}, f32[]{:T(128)}) all-reduce(f32[]{:T(128)} %get-tuple-element.120, f32[]{:T(128)} %get-tuple-element.119), channel_id=1, replica_groups=mesh['ent'=2,'blk'=4,'rel'=4] {'ent','blk','rel'}, use_global_device_ids=true, to_apply=%region_21.22 | all-reduce | flops 2 | bytes 16 | tf_op jit(solution)/shard_map/psum | solution.py:21
  343.4 0.1 multiply_subtract_fusion.3
  343.5 0.6 convolution_bitcast_fusion.5
  344.1 1.3 multiply_reduce_fusion.4
  345.4 41.3 %all-reduce.2 = (f32[]{:T(128)}, f32[]{:T(128)}) all-reduce(f32[]{:T(128)} %get-tuple-element.118, f32[]{:T(128)} %get-tuple-element.117), channel_id=1, replica_groups=mesh['ent'=2,'blk'=4,'rel'=4] {'ent','blk','rel'}, use_global_device_ids=true, to_apply=%region_25.26 | all-reduce | flops 2 | bytes 16 | tf_op jit(solution)/shard_map/psum | solution.py:21
  390.7 0.1 multiply_subtract_fusion.2
  390.7 0.6 convolution_bitcast_fusion.3
  391.3 1.2 multiply_reduce_fusion.2
  392.5 39.5 %all-reduce.1 = (f32[]{:T(128)}, f32[]{:T(128)}) all-reduce(f32[]{:T(128)} %get-tuple-element.116, f32[]{:T(128)} %get-tuple-element.115), channel_id=1, replica_groups=mesh['ent'=2,'blk'=4,'rel'=4] {'ent','blk','rel'}, use_global_device_ids=true, to_apply=%region_29.30 | all-reduce | flops 2 | bytes 16 | tf_op jit(solution)/shard_map/psum | solution.py:21
  436.0 0.0 copy-start.2
  436.0 0.1 multiply_subtract_fusion.1
  436.1 0.6 convolution_bitcast_fusion.1
  436.7 1.3 multiply_reduce_fusion
  437.9 41.3 %all-reduce = (f32[]{:T(128)}, f32[]{:T(128)}) all-reduce(f32[]{:T(128)} %get-tuple-element.114, f32[]{:T(128)} %get-tuple-element.113), channel_id=1, replica_groups=mesh['ent'=2,'blk'=4,'rel'=4] {'ent','blk','rel'}, use_global_device_ids=true, to_apply=%region_33.34 | all-reduce | flops 2 | bytes 16 | tf_op jit(solution)/shard_map/psum | solution.py:21
  483.2 0.8 multiply_subtract_fusion
  484.0 0.0 copy-done.2
  484.0 1.0 multiply_add_fusion
  (19 shorter events, 0.1 us)
Async XLA Ops:
  7.2 4.2 copy-start.1
  7.2 4.5 copy-start.3
  7.2 61.1 %all-reduce.10.cloned.1.call-start = ((), (), s32[]{:S(2)}) async-start(), calls=%async_computation.2 | async-start | bytes 524288 | tf_op jit(solution)/shard_map/psum | solution.py:52
  9.5 102.6 %reduce-scatter.2.cloned.1.call-start = ((), (), s32[]{:S(2)}) async-start(), calls=%async_computation.1 | async-start | bytes 2359296 | tf_op jit(solution)/shard_map/reduce_scatter | solution.py:84
  68.3 89.5 %copy-start = (f32[256,256]{1,0:T(8,128)S(1)}, f32[256,256]{1,0:T(8,128)}, u32[]{:S(2)}) copy-start(f32[256,256]{1,0:T(8,128)} %all-reduce.10.cloned.1.call-done) | copy-start | bytes 786436
  436.0 48.0 %copy-start.2 = (f32[1,256,256]{2,1,0:T(8,128)S(1)}, f32[1,256,256]{2,1,0:T(8,128)}, u32[]{:S(2)}) copy-start(f32[1,256,256]{2,1,0:T(8,128)} %reduce-scatter.2.cloned.1.call-done) | copy-start | bytes 786436
Sparse Core Ops, SparseCore 0:
  11.6 56.6 all-reduce.9
  71.6 40.4 reduce-scatter.1
where the time goes:
time: 494 us; the launch traced here: 492 us
  blocking collectives  324 us (66%)
  waiting for transfers between devices  82.8 us (17%)
  between operations  43.5 us (9%)
  matrix products  35.6 us (7%)
  other arithmetic  5.49 us (1%)
    psum x8, blocking collectives, two_products(): lax.psum((jnp.sum(residual * residual), jnp.sum(residual * image_map)), (...  324 us
    reduce_scatter x1, waiting for transfers between devices, body(): lax.psum_scatter(results.reshape(own_rows * lax.axis_size(('ent', 'blk'))...  43.8 us
    psum x1, waiting for transfers between devices, body(): lax.psum(jnp.dot(factors.T, factors, preferred_element_type=jnp.float32),...  39 us
    dot_general x8, matrix products, apply_normal(): jnp.einsum('kac,cd->kad', left_side, gram_matrix, precision=lax.Precision...  10.9 us
  transfers between devices with their start and end apart: 2, of which 2 were waited for; matrix products, arithmetic and copies ran while one was open for 4% of the time, Pallas kernels for 0%

commit v1 on v0

--- a/solution.py
+++ b/solution.py
@@ -49,9 +49,9 @@
     triple_count = heads.shape[3]
     relation_rows = heads.shape[0] * heads.shape[2]
     norm_scale = 1.0 / math.sqrt(shards * triple_count)
-    gram_total = lax.psum(
-        jnp.dot(factors.T, factors, preferred_element_type=jnp.float32), ("ent", "blk")
-    )
+    part = jnp.dot(factors.T, factors, preferred_element_type=jnp.float32)
+    parts = lax.all_gather(part, ("ent", "blk"))
+    gram_total = jnp.sum(parts, axis=0)
     gram_matrix = gram_total / (ent_dev * shards)
     block_table = factors.reshape(ent_dev // tile_width, tile_width, rank_width)
     head_ids = heads.reshape(relation_rows, triple_count)

time: 494 us -> 466 us (0.943)
  waiting for transfers between devices: 82.8 us -> 54.4 us
    psum x1 -> x0, waiting for transfers between devices: 39 us -> none  [body(): lax.psum(jnp.dot(factors.T, factors, preferred_element_type=jnp.float32),...]
    all_gather x0 -> x1, waiting for transfers between devices: none -> 11.7 us  [body(): parts = lax.all_gather(part, ('ent', 'blk'))]
  transfers between devices with their start and end apart: 2 -> 2, of which waited for: 2 -> 2; matrix products, arithmetic and copies ran while one was open for 4% -> 5% of each run, Pallas kernels for 0% -> 0%
where the time goes in v1:
time: 466 us; the launch traced here: 464 us
  blocking collectives  324 us (70%)
  waiting for transfers between devices  54.4 us (12%)
  between operations  42.9 us (9%)
  matrix products  35.6 us (8%)
  other arithmetic  7.25 us (2%)
    psum x8, blocking collectives, two_products(): lax.psum((jnp.sum(residual * residual), jnp.sum(residual * image_map)), (...  324 us
    reduce_scatter x1, waiting for transfers between devices, body(): lax.psum_scatter(results.reshape(own_rows * lax.axis_size(('ent', 'blk'))...  42.7 us
    all_gather x1, waiting for transfers between devices, body(): parts = lax.all_gather(part, ('ent', 'blk'))  11.7 us
    dot_general x8, matrix products, apply_normal(): jnp.einsum('kac,cd->kad', left_side, gram_matrix, precision=lax.Precision...  10.9 us
  transfers between devices with their start and end apart: 2, of which 2 were waited for; matrix products, arithmetic and copies ran while one was open for 5% of the time, Pallas kernels for 0%

profile of v1, /device:TPU:0, one launch (start us, length us, event | category | flops | bytes accessed | tf_op | source)
XLA Modules:
  0.0 464.3 jit_solution(4138317408375631745)
XLA Ops:
  7.2 0.0 copy-start
  7.2 0.0 copy-start.2
  7.2 0.0 all-gather.3.cloned.1.call-start
  7.2 2.3 fusion.80
  9.5 0.0 all-gather.3.cloned.1.call-update
  9.5 0.0 reduce-scatter.2.cloned.1.call-start
  9.6 0.8 reduce.2
  10.5 0.8 reduce.3
  11.3 0.0 copy-done
  11.3 0.3 copy.14
  11.6 0.0 copy-done.2
  11.6 0.1 reduce.4
  11.7 17.5 %while.13 = (s32[]{:T(128)}, f32[2,4,256,256]{3,2,1,0:T(8,128)}, f32[2,4,1024]{2,1,0:T(4,128)S(1)}, s32[2,4,1024]{2,1,0:T(4,128)S(1)}, bf16[8,128,256]{2,0,1:T(8...) while((s32[]{:T(128)}, f32[2,4,256,256]{3,2,1,0:T(8,128)}, f32[2,4,1024]{2,1,0:T(4,128)S(1)}, ...), condition=%wide.region_1.2_spmd, body=%wide.region_0.0_spmd.sunk | while | flops 1113941504 | bytes 14992225 | solution.py:83
  11.8 0.2 fusion.111
  11.9 0.7 convolution_convert_fusion.4
  12.7 2.7 multiply_convert_fusion.2
  15.5 0.2 fusion.112
  15.6 0.7 convolution_convert_fusion.5
  16.4 4.1 fusion.113
  20.5 0.2 fusion.111
  20.7 0.7 convolution_convert_fusion.4
  21.5 2.7 multiply_convert_fusion.2
  24.2 0.2 fusion.112
  24.4 0.7 convolution_convert_fusion.5
  25.1 4.1 fusion.113
  29.3 0.0 reduce-scatter.2.cloned.1.call-update
  29.3 11.7 %all-gather.3.cloned.1.call-done = f32[2048,256]{1,0:T(8,128)} async-done(((f32[256,256]{1,0:T(8,128)}), f32[2048,256]{1,0:T(8,128)}) %all-gather.3.cloned.1.call-update) | async-done | bytes 2097168 | tf_op jit(solution)/shard_map/all_gather | solution.py:53
  41.0 1.8 reduce_sum.154
  42.8 42.7 %reduce-scatter.2.cloned.1.call-done = f32[1,256,256]{2,1,0:T(8,128)} async-done(((f32[8,256,256]{2,1,0:T(8,128)}), f32[1,256,256]{2,1,0:T(8,128)}) %reduce-scatter.2.cloned.1.call-update) | async-done | bytes 262160 | tf_op jit(solution)/shard_map/reduce_scatter | solution.py:84
  85.4 1.5 convolution_bitcast_fusion.15
  87.0 2.2 multiply_reduce_fusion.14
  89.1 39.5 %all-reduce.7 = (f32[]{:T(128)}, f32[]{:T(128)}) all-reduce(f32[]{:T(128)} %get-tuple-element.128, f32[]{:T(128)} %get-tuple-element.127), channel_id=1, replica_groups=mesh['ent'=2,'blk'=4,'rel'=4] {'ent','blk','rel'}, use_global_device_ids=true, to_apply=%region_4.5 | all-reduce | flops 2 | bytes 16 | tf_op jit(solution)/shard_map/psum | solution.py:21
  130.0 1.0 multiply_subtract_fusion.7
  131.0 0.6 convolution_bitcast_fusion.13
  131.6 1.3 multiply_reduce_fusion.12
  132.8 41.4 %all-reduce.6 = (f32[]{:T(128)}, f32[]{:T(128)}) all-reduce(f32[]{:T(128)} %get-tuple-element.126, f32[]{:T(128)} %get-tuple-element.125), channel_id=1, replica_groups=mesh['ent'=2,'blk'=4,'rel'=4] {'ent','blk','rel'}, use_global_device_ids=true, to_apply=%region_9.10 | all-reduce | flops 2 | bytes 16 | tf_op jit(solution)/shard_map/psum | solution.py:21
  178.8 0.1 multiply_subtract_fusion.6
  178.9 0.6 convolution_bitcast_fusion.11
  179.5 1.2 multiply_reduce_fusion.10
  180.7 39.5 %all-reduce.5 = (f32[]{:T(128)}, f32[]{:T(128)}) all-reduce(f32[]{:T(128)} %get-tuple-element.124, f32[]{:T(128)} %get-tuple-element.123), channel_id=1, replica_groups=mesh['ent'=2,'blk'=4,'rel'=4] {'ent','blk','rel'}, use_global_device_ids=true, to_apply=%region_13.14 | all-reduce | flops 2 | bytes 16 | tf_op jit(solution)/shard_map/psum | solution.py:21
  224.1 0.1 multiply_subtract_fusion.5
  224.2 0.6 convolution_bitcast_fusion.9
  224.8 1.3 multiply_reduce_fusion.8
  226.1 41.5 %all-reduce.4 = (f32[]{:T(128)}, f32[]{:T(128)}) all-reduce(f32[]{:T(128)} %get-tuple-element.122, f32[]{:T(128)} %get-tuple-element.121), channel_id=1, replica_groups=mesh['ent'=2,'blk'=4,'rel'=4] {'ent','blk','rel'}, use_global_device_ids=true, to_apply=%region_17.18 | all-reduce | flops 2 | bytes 16 | tf_op jit(solution)/shard_map/psum | solution.py:21
  271.3 0.1 multiply_subtract_fusion.4
  271.4 0.6 convolution_bitcast_fusion.7
  272.0 1.2 multiply_reduce_fusion.6
  273.2 39.5 %all-reduce.3 = (f32[]{:T(128)}, f32[]{:T(128)}) all-reduce(f32[]{:T(128)} %get-tuple-element.120, f32[]{:T(128)} %get-tuple-element.119), channel_id=1, replica_groups=mesh['ent'=2,'blk'=4,'rel'=4] {'ent','blk','rel'}, use_global_device_ids=true, to_apply=%region_21.22 | all-reduce | flops 2 | bytes 16 | tf_op jit(solution)/shard_map/psum | solution.py:21
  316.5 0.1 multiply_subtract_fusion.3
  316.6 0.6 convolution_bitcast_fusion.5
  317.2 1.3 multiply_reduce_fusion.4
  318.5 41.3 %all-reduce.2 = (f32[]{:T(128)}, f32[]{:T(128)}) all-reduce(f32[]{:T(128)} %get-tuple-element.118, f32[]{:T(128)} %get-tuple-element.117), channel_id=1, replica_groups=mesh['ent'=2,'blk'=4,'rel'=4] {'ent','blk','rel'}, use_global_device_ids=true, to_apply=%region_25.26 | all-reduce | flops 2 | bytes 16 | tf_op jit(solution)/shard_map/psum | solution.py:21
  363.6 0.1 multiply_subtract_fusion.2
  363.6 0.6 convolution_bitcast_fusion.3
  364.2 1.2 multiply_reduce_fusion.2
  365.4 39.5 %all-reduce.1 = (f32[]{:T(128)}, f32[]{:T(128)}) all-reduce(f32[]{:T(128)} %get-tuple-element.116, f32[]{:T(128)} %get-tuple-element.115), channel_id=1, replica_groups=mesh['ent'=2,'blk'=4,'rel'=4] {'ent','blk','rel'}, use_global_device_ids=true, to_apply=%region_29.30 | all-reduce | flops 2 | bytes 16 | tf_op jit(solution)/shard_map/psum | solution.py:21
  408.7 0.0 copy-start.1
  408.7 0.1 multiply_subtract_fusion.1
  408.8 0.6 convolution_bitcast_fusion.1
  409.4 1.3 multiply_reduce_fusion
  410.7 41.3 %all-reduce = (f32[]{:T(128)}, f32[]{:T(128)}) all-reduce(f32[]{:T(128)} %get-tuple-element.114, f32[]{:T(128)} %get-tuple-element.113), channel_id=1, replica_groups=mesh['ent'=2,'blk'=4,'rel'=4] {'ent','blk','rel'}, use_global_device_ids=true, to_apply=%region_33.34 | all-reduce | flops 2 | bytes 16 | tf_op jit(solution)/shard_map/psum | solution.py:21
  455.7 0.8 multiply_subtract_fusion
  456.5 0.0 copy-done.1
  456.5 1.0 multiply_add_fusion
  (18 shorter events, 0.1 us)
Async XLA Ops:
  7.2 4.2 copy-start
  7.2 4.5 copy-start.2
  7.2 33.8 %all-gather.3.cloned.1.call-start = ((), (), s32[]{:S(2)}) async-start(), calls=%async_computation.2 | async-start | bytes 2359296 | tf_op jit(solution)/shard_map/all_gather | solution.py:53
  9.5 75.9 %reduce-scatter.2.cloned.1.call-start = ((), (), s32[]{:S(2)}) async-start(), calls=%async_computation.1 | async-start | bytes 2359296 | tf_op jit(solution)/shard_map/reduce_scatter | solution.py:84
  408.7 47.8 %copy-start.1 = (f32[1,256,256]{2,1,0:T(8,128)S(1)}, f32[1,256,256]{2,1,0:T(8,128)}, u32[]{:S(2)}) copy-start(f32[1,256,256]{2,1,0:T(8,128)} %reduce-scatter.2.cloned.1.call-done) | copy-start | bytes 786436
Sparse Core Ops, SparseCore 0:
  10.5 30.4 all-gather.2
  44.3 41.0 reduce-scatter.1
